TPU v7x, 32 devices: a whole 2x2x4 slice. The times are simulated.
32 devices in a mesh: lon: 16 (over z, y, x), lev: 2 (over core).
Axes of the slice: x: 2, y: 2, z: 4, core: 2. Of those that a mesh axis runs over, the one named last changes fastest.
Arguments:
- ensemble: float32 [80, 16, 16384], P(None, 'lev', 'lon'), may hold values from -6 to 6
- obs_cell: int32 [12, 128], P(None, 'lon'), may hold values from 0 to 16383, as said below
- obs_value: float32 [12, 128], P(None, 'lon'), may hold values from -5 to 5
- obs_noise: float32 [12, 128], P(None, 'lon'), may hold values from 0.2 to 2
- obs_weight: float32 [12, 16, 128], P(None, 'lev'), may hold values from 0.05 to 0.5
- tile_lists: int32 [12, 384], P(None, 'lon'), may hold values from 0 to 128, as said below
- batch_order: int32 [12], replicated, may hold values from 0 to 11, each once
Outputs:
- analysis: float32 [80, 16, 16384], P(None, 'lev', 'lon')
Inputs may be any that keep to these rules, and one draw needn't show every extreme that they name: `obs_cell`: each tile holds at most 8 observations of one block, and some tile exactly 8. `tile_lists`: for block b and tile t the tile's 24 slots hold first, ascending and once each, the observations of block b whose tile is t or a neighbour of t around the globe, then the value 128 in every remaining slot; in every block some tile has all 24 slots used. `batch_order`: each block once.
All inputs are finite; a program needn't handle non-finite values.
Results may differ from a plain program's by a relative error of at most 0.0003.
Values sent between devices are 32-bit elements; how exact they have to be, the bound alone decides.
A program may use at most 128 MiB of HBM per device.

v0:
```python
import functools

import jax
import jax.numpy as jnp
from jax import lax
from jax.experimental import pallas as pl
from jax.experimental.pallas import tpu as pltpu
from jax.sharding import PartitionSpec as P

LON_DEV = 16
CELL_DEV = 1024
PANEL = 8

highest = lax.Precision.HIGHEST
f32 = jnp.float32
bf16 = jnp.bfloat16


def split(x):
    high = x.astype(bf16)
    low = (x - high.astype(f32)).astype(bf16)
    return high, low


def dot(a, b):
    return jnp.dot(a, b, preferred_element_type=f32)


def tapered_weight(row_a, col_a, row_c, col_c, circle):
    e = jnp.abs(col_a - col_c)
    e = jnp.minimum(e, circle - e)
    d = row_a - row_c
    return jnp.exp((e * e + d * d) * (-2.0 / (LON_DEV * LON_DEV)))


def eliminate(a_ref, b_ref, noise_root, mem, obs, width):
    lane = lax.broadcasted_iota(jnp.int32, (1, obs), 1)
    sample = lax.broadcasted_iota(jnp.int32, (1, width), 1) < mem
    for start in range(0, obs, PANEL):
        spot = [[None] * PANEL for _ in range(PANEL)]
        for i in range(PANEL):
            for s in range(i + 1):
                spot[i][s] = jnp.broadcast_to(
                    a_ref[start + i : start + i + 1, start + s : start + s + 1], (1, obs)
                )
        in_panel = (lane >= start) & (lane < start + PANEL)
        rows = []
        sides = []
        for i in range(PANEL):
            row = a_ref[start + i : start + i + 1, :]
            rows.append(jnp.where(in_panel, jnp.where(lane == start + i, 1.0, 0.0), row))
            sides.append(b_ref[start + i : start + i + 1, :])
        scaled_rows = []
        scaled_sides = []
        for r in range(PANEL):
            pivot = spot[r][r]
            inverse_root = lax.rsqrt(pivot)
            inverse = inverse_root * inverse_root
            root = pivot * inverse_root
            added = jnp.where(sample, noise_root[start + r], 0.0)
            factor = 1.0 / (root + added)
            below = [spot[i][r] * inverse for i in range(r + 1, PANEL)]
            for n, i in enumerate(range(r + 1, PANEL)):
                for s in range(r + 1, i + 1):
                    spot[i][s] = spot[i][s] - below[n] * spot[s][r]
            solved = sides[r] * factor
            passing = solved * root
            for n, i in enumerate(range(r + 1, PANEL)):
                rows[i] = rows[i] - below[n] * rows[r]
                sides[i] = sides[i] - below[n] * passing
            scaled_rows.append(rows[r] * inverse)
            scaled_sides.append(solved * inverse_root)
            a_ref[start + r : start + r + 1, :] = jnp.where(
                lane < start + PANEL, rows[r] * inverse_root, 0.0
            )
            b_ref[start + r : start + r + 1, :] = solved
        after = start + PANEL
        if after < obs:
            upper = jnp.concatenate(rows, axis=0)
            left = upper.T[after:, :]
            right = jnp.concatenate(
                [jnp.concatenate(scaled_rows, axis=0), jnp.concatenate(scaled_sides, axis=0)], axis=1
            )
            change = jnp.dot(left, right, precision=highest, preferred_element_type=f32)
            a_ref[after:, :] = jnp.where(in_panel, 0.0, a_ref[after:, :]) - change[:, :obs]
            b_ref[after:, :] = b_ref[after:, :] - change[:, obs:]


def kernel_body(
    x_ref, probe_ref, value_ref, noise_ref, noise_col_ref, cell_row_ref, cell_col_ref, list_ref,
    out_ref, probes, a_ref, b_ref, *, batches, levels, mem, obs, cells, slots, axis_size,
):
    tile = lax.axis_index("lon")
    circle = float(LON_DEV * axis_size)
    scale = 1.0 / (mem - 1)
    probes[...] = probe_ref[...]
    cell = lax.broadcasted_iota(jnp.int32, (1, cells), 1)
    here_row = (cell // LON_DEV).astype(f32)
    here_col = (tile * LON_DEV + cell % LON_DEV).astype(f32)
    target = cell_row_ref[...]
    target_tile = target // CELL_DEV
    target_within = target - target_tile * CELL_DEV
    target_row_int = target_within // LON_DEV
    target_col = (target_tile * LON_DEV + target_within - target_row_int * LON_DEV).astype(f32)
    target_row = target_row_int.astype(f32)
    target_tile = target_tile.astype(f32)
    lanes = lax.broadcasted_iota(jnp.int32, (obs, obs), 1)
    subs = lax.broadcasted_iota(jnp.int32, (obs, obs), 0)

    def turn(k, carry):
        now = probes[k]
        centre = jnp.mean(now, axis=0, keepdims=True)
        spread = now - centre
        innovation = value_ref[k] - centre
        padded = jnp.concatenate(
            [spread, innovation, jnp.zeros((obs - mem - 1, obs), f32)], axis=0
        )
        sides = padded.T
        noise_row = noise_ref[k]
        covariance = jnp.dot(sides[:, :mem], spread, precision=highest, preferred_element_type=f32) * scale
        a_ref[...] = covariance + jnp.where(lanes == subs, noise_row, 0.0)
        b_ref[...] = sides
        root_col = jnp.sqrt(noise_col_ref[k])
        roots = [root_col[j : j + 1, :] for j in range(obs)]
        eliminate(a_ref, b_ref, roots, mem, obs, obs)
        joined = lax.dot_general(
            a_ref[...], b_ref[...], (((0,), (0,)), ((), ())), precision=highest, preferred_element_type=f32
        )
        gain_t = joined[:, mem : mem + 1] - joined
        gain = gain_t.T[:mem, :]

        s_high, s_low = split(spread)
        stacked = jnp.concatenate([s_high.astype(f32), s_high.astype(f32), s_low.astype(f32)], axis=0)
        left = stacked.T.astype(bf16)
        g_high, g_low = split(gain)
        gains = jnp.concatenate([g_high, g_high, g_low], axis=1)

        cell_col = cell_col_ref[k]
        from_tile = cell_col // CELL_DEV
        from_within = cell_col - from_tile * CELL_DEV
        from_row = from_within // LON_DEV
        from_col = (from_tile * LON_DEV + from_within - from_row * LON_DEV).astype(f32)
        from_row = from_row.astype(f32)
        from_tile = from_tile.astype(f32)

        def renew(b, carry):
            @pl.when(2 * b + 1 > k)
            def _():
                upcoming = jnp.concatenate([probes[2 * b], probes[2 * b + 1]], axis=1)
                high, low = split(upcoming)
                crossed = dot(left, jnp.concatenate([high, low, high], axis=0))
                weights = []
                for u in range(2):
                    weight = tapered_weight(
                        from_row, from_col, target_row_ref_get(b, u), target_col_ref_get(b, u), circle
                    )
                    apart = jnp.abs(from_tile - target_tile_ref_get(b, u))
                    near = (apart < 1.5) | (apart > axis_size - 1.5)
                    weights.append(jnp.where(near, weight * scale, 0.0))
                tapered = crossed * jnp.concatenate(weights, axis=1)
                high, low = split(tapered)
                upcoming = upcoming + dot(gains, jnp.concatenate([high, low, high], axis=0))
                probes[2 * b] = upcoming[:, :obs]
                probes[2 * b + 1] = upcoming[:, obs:]

            return carry

        def target_row_ref_get(b, u):
            return target_row[2 * b + u]

        def target_col_ref_get(b, u):
            return target_col[2 * b + u]

        def target_tile_ref_get(b, u):
            return target_tile[2 * b + u]

        for b in range(batches // 2):
            renew(b, 0)

        listed = list_ref[k]
        chosen = lanes[:slots] == listed
        select = chosen.astype(bf16)
        pick_row = cell_row_ref[k]
        pick_tile = pick_row // CELL_DEV
        pick_within = pick_row - pick_tile * CELL_DEV
        pick_r = pick_within // LON_DEV
        pick_c = (pick_tile * LON_DEV + pick_within - pick_r * LON_DEV).astype(f32)
        list_row = jnp.sum(jnp.where(chosen, pick_r.astype(f32), 0.0), axis=1, keepdims=True)
        list_col = jnp.sum(jnp.where(chosen, pick_c, 0.0), axis=1, keepdims=True)
        usable = jnp.where(listed < obs, scale, 0.0)
        weight = tapered_weight(list_row, list_col, here_row, here_col, circle) * usable
        left_listed = dot(select, left).astype(bf16)
        gt_high, gt_low = split(gain_t)
        gt_high = dot(select, gt_high)
        gt_low = dot(select, gt_low)
        gains_listed = jnp.concatenate([gt_high, gt_high, gt_low, jnp.zeros((obs - 3 * slots, obs), f32)], axis=0)
        gains_listed = gains_listed.T[:mem, : 3 * slots].astype(bf16)

        def spread_level(level, carry, source):
            block = source[level]
            high, low = split(block)
            crossed = dot(left_listed, jnp.concatenate([high, low, high], axis=0))
            high, low = split(crossed * weight)
            out_ref[level] = block + dot(gains_listed, jnp.concatenate([high, low, high], axis=0))
            return carry

        lax.fori_loop(0, levels, functools.partial(spread_level, source=out_ref), 0)
        return carry

    out_ref[...] = x_ref[...]
    lax.fori_loop(0, batches, turn, 0)


def peer_of(d, ranks, both):
    lon, lev = lax.axis_index("lon"), lax.axis_index("lev")
    if not both:
        return lax.rem(lon + d, ranks), lev
    cores = lax.axis_size("lev")
    number = lax.rem(lon * cores + lev + d, ranks)
    return lax.div(number, cores), lax.rem(number, cores)


def meet(ranks, both):
    barrier = pltpu.get_barrier_semaphore()

    def announce(d, carry):
        pl.semaphore_signal(
            barrier, inc=1, device_id=peer_of(d, ranks, both), device_id_type=pl.DeviceIdType.MESH
        )
        return carry

    lax.fori_loop(1, ranks, announce, 0)
    pl.semaphore_wait(barrier, ranks - 1)


def each_peer(ranks, copy_to):
    def start(d, carry):
        copy_to(d).start()
        return carry

    def finish(d, carry):
        copy_to(d).wait()
        return carry

    return (
        lambda: lax.fori_loop(1, ranks, start, 0),
        lambda: lax.fori_loop(1, ranks, finish, 0),
    )


def table_kernel(mine_ref, out_ref, landed, send_sem, recv_sem, *, ranks):
    meet(ranks, False)

    def copy_to(d):
        return pltpu.make_async_remote_copy(
            src_ref=mine_ref,
            dst_ref=landed.at[d],
            send_sem=send_sem.at[d],
            recv_sem=recv_sem.at[d],
            device_id=peer_of(d, ranks, False),
            device_id_type=pl.DeviceIdType.MESH,
        )

    start, finish = each_peer(ranks, copy_to)
    start()
    landed[0] = mine_ref[...]
    finish()
    out_ref[...] = jnp.sum(landed[...], axis=0)


def sum_kernel(mine_ref, out_ref, landed, total, send_sem, recv_sem, send_again, recv_again, *, ranks, rows):
    meet(ranks, True)
    me = lax.axis_index("lon") * lax.axis_size("lev") + lax.axis_index("lev")
    own = pl.ds(pl.multiple_of(me * rows, rows), rows)

    def scatter_to(d):
        other = lax.rem(me + d, ranks)
        return pltpu.make_async_remote_copy(
            src_ref=mine_ref.at[pl.ds(pl.multiple_of(other * rows, rows), rows)],
            dst_ref=landed.at[d],
            send_sem=send_sem.at[d],
            recv_sem=recv_sem.at[d],
            device_id=peer_of(d, ranks, True),
            device_id_type=pl.DeviceIdType.MESH,
        )

    def gather_to(d):
        return pltpu.make_async_remote_copy(
            src_ref=total,
            dst_ref=out_ref.at[own],
            send_sem=send_again.at[d],
            recv_sem=recv_again.at[d],
            device_id=peer_of(d, ranks, True),
            device_id_type=pl.DeviceIdType.MESH,
        )

    start, finish = each_peer(ranks, scatter_to)
    start()
    landed[0] = mine_ref[own]
    finish()
    total[...] = jnp.sum(landed[...], axis=0)
    start, finish = each_peer(ranks, gather_to)
    start()
    out_ref[own] = total[...]
    finish()


def gathered_table(parts, axis_size):
    rows, own = parts.shape
    padded = -(-rows // 8) * 8
    width = own * axis_size
    lane = jnp.arange(width, dtype=jnp.int32)[None, :]
    placed = jnp.where(lane // own == lax.axis_index("lon"), jnp.tile(parts, (1, axis_size)), 0.0)
    placed = jnp.pad(placed, ((0, padded - rows), (0, 0)))
    return pl.pallas_call(
        functools.partial(table_kernel, ranks=axis_size),
        out_shape=jax.ShapeDtypeStruct((padded, width), f32),
        in_specs=[pl.BlockSpec(memory_space=pltpu.VMEM)],
        out_specs=pl.BlockSpec(memory_space=pltpu.VMEM),
        scratch_shapes=[
            pltpu.VMEM((axis_size, padded, width), f32),
            pltpu.SemaphoreType.DMA((axis_size,)),
            pltpu.SemaphoreType.DMA((axis_size,)),
        ],
        compiler_params=pltpu.CompilerParams(collective_id=0, has_side_effects=True),
        name="table",
    )(placed)[:rows]


def summed(portions, ranks):
    count, width = portions.shape
    rows = -(-count // (8 * ranks)) * 8
    padded = jnp.pad(portions, ((0, rows * ranks - count), (0, 0)))
    return pl.pallas_call(
        functools.partial(sum_kernel, ranks=ranks, rows=rows),
        out_shape=jax.ShapeDtypeStruct(padded.shape, f32),
        in_specs=[pl.BlockSpec(memory_space=pltpu.VMEM)],
        out_specs=pl.BlockSpec(memory_space=pltpu.VMEM),
        scratch_shapes=[
            pltpu.VMEM((ranks, rows, width), f32),
            pltpu.VMEM((rows, width), f32),
            pltpu.SemaphoreType.DMA((ranks,)),
            pltpu.SemaphoreType.DMA((ranks,)),
            pltpu.SemaphoreType.DMA((ranks,)),
            pltpu.SemaphoreType.DMA((ranks,)),
        ],
        compiler_params=pltpu.CompilerParams(collective_id=1, has_side_effects=True),
        name="total",
    )(padded)[:count]


def body(ensemble, obs_cell, obs_value, obs_noise, obs_weight, tile_lists, batch_order):
    mem, levels, cells = ensemble.shape
    batches = obs_cell.shape[0]
    axis_size = lax.axis_size("lon")
    obs = obs_cell.shape[1] * axis_size
    slots = 32
    parts = jnp.concatenate([obs_cell.astype(f32), obs_value, obs_noise], axis=0)
    table = gathered_table(parts, axis_size)
    cell_table = table[:batches].astype(jnp.int32)
    observed = table[batches : 2 * batches]
    noise = table[2 * batches :]
    offset = lax.axis_index("lon") * CELL_DEV

    cell_table = cell_table[batch_order]
    observed = observed[batch_order]
    noise = noise[batch_order]
    weights = obs_weight[batch_order]
    lists = tile_lists[batch_order]

    owned = ((cell_table >= offset) & (cell_table < offset + CELL_DEV)).astype(f32)
    within = jnp.clip(cell_table - offset, 0, CELL_DEV - 1)

    def portion_of(inside, mine, weight):
        picked = jnp.take(ensemble, inside, axis=2)
        return jnp.sum(picked * (weight * mine[None, :])[None], axis=1)

    portions = jax.vmap(portion_of)(within, owned, weights).reshape(batches * mem, obs)
    probes = summed(portions, axis_size * lax.axis_size("lev")).reshape(batches, mem, obs)
    lists = jnp.pad(lists, ((0, 0), (0, slots - lists.shape[1])), constant_values=obs)

    call = pl.pallas_call(
        functools.partial(
            kernel_body, batches=batches, levels=levels, mem=mem, obs=obs, cells=cells, slots=slots,
            axis_size=axis_size,
        ),
        out_shape=jax.ShapeDtypeStruct((levels, mem, cells), f32),
        in_specs=[pl.BlockSpec(memory_space=pltpu.VMEM)] * 8,
        out_specs=pl.BlockSpec(memory_space=pltpu.VMEM),
        scratch_shapes=[
            pltpu.VMEM((batches, mem, obs), f32),
            pltpu.VMEM((obs, obs), f32),
            pltpu.VMEM((obs, obs), f32),
        ],
        compiler_params=pltpu.CompilerParams(vmem_limit_bytes=40 * 1024 * 1024),
        name="assimilate",
    )
    out = call(
        ensemble.transpose(1, 0, 2),
        probes,
        observed[:, None, :],
        noise[:, None, :],
        noise[:, :, None],
        cell_table[:, None, :],
        cell_table[:, :, None],
        lists[:, :, None],
    )
    return out.transpose(1, 0, 2)


def solution(mesh):
    return jax.shard_map(
        body,
        mesh=mesh,
        in_specs=(
            P(None, "lev", "lon"),
            P(None, "lon"),
            P(None, "lon"),
            P(None, "lon"),
            P(None, "lev", None),
            P(None, "lon"),
            P(),
        ),
        out_specs=P(None, "lev", "lon"),
        check_vma=False,
    )
```

profile of v0, /device:TPU:9, one launch (start us, length us, event | category | flops | bytes accessed | tf_op | source)
XLA Modules:
  0.0 220.4 jit_solution(4745250013141297891)
XLA Ops:
  0.0 0.0 copy-start
  0.0 0.7 compare_select_fusion.2
  0.7 0.7 convert_element_type.17
  1.4 0.8 pad_maximum_fusion
  2.2 0.1 copy.20
  2.2 0.6 pad.12.mine_ref
  2.9 13.0 %table.1 = f32[40,128]{1,0:T(8,128)} custom-call(f32[40,128]{1,0:T(8,128)} %pad.12.mine_ref), custom_call_target="tpu_custom_call" | custom-call | tf_op jit(solution)/shard_map/table/pallas_call | solution.py:315
  15.9 0.8 fusion.3
  16.6 0.6 gather_fusion
  17.2 0.0 copy-done
  17.2 0.6 gather_fusion.2
  17.8 0.3 copy.22
  18.1 4.7 %copy.21 = f32[80,8,1024]{0,1,2:T(8,128)} copy(f32[80,8,1024]{2,1,0:T(8,128)} %param.7) | data formatting | bytes 5242880 | tf_op args[0]
  22.9 6.7 %gather_fusion.1 = f32[1536,80,8]{1,2,0:T(8,128)} fusion(f32[80,8,1024]{0,1,2:T(8,128)} %copy.21, s32[2048]{0:T(1024)S(1)} %pad_clamp_fusion), kind=kCustom, calls=%fused_computation.1 | custom fusion | bytes 7870464 | tf_op jit(solution)/shard_map/vmap(jit(_take))/gather | solution.py:375
  29.5 0.0 copy-start.1
  29.5 5.4 %fusion = f32[12,80,128]{1,2,0:T(8,128)S(1)} fusion(f32[12,128,80,8]{2,3,1,0:T(8,128)} %bitcast.23, f32[12,8,128]{1,2,0:T(8,128)S(1)} %copy.22, pred[12,128]{1,0:T(8,128)(4,1)S(1)} %get-tuple-element.8), kind=kLoop, calls=%fused_computation.7 | loop fusion | flops 2826240 | bytes 4474368 | tf_op jit(solution)/shard_map/vmap()/reduce_sum | solution.py:376
  35.0 0.3 copy.23
  35.2 0.8 pad.13.mine_ref
  36.1 31.6 %total.1 = f32[1024,128]{1,0:T(8,128)} custom-call(f32[1024,128]{1,0:T(8,128)} %pad.13.mine_ref), custom_call_target="tpu_custom_call" | custom-call | tf_op jit(solution)/shard_map/total/pallas_call | solution.py:334
  67.7 1.1 slice.17
  68.8 0.3 copy.25.cell_col_ref
  69.1 0.6 gather_fusion.4
  69.7 0.3 copy.24.noise_col_ref
  70.0 0.6 gather_fusion.3
  70.5 0.0 copy-done.1
  70.6 0.6 gather_fusion.5
  71.1 0.2 copy.26.list_ref
  71.3 3.3 %copy.29 = f32[80,8,1024]{2,0,1:T(8,128)S(1)} copy(f32[80,8,1024]{2,1,0:T(8,128)} %param.7) | data formatting | bytes 5242880 | tf_op args[0]
  74.5 142.8 %assimilate.1 = f32[8,80,1024]{2,1,0:T(8,128)S(1)} custom-call(f32[8,80,1024]{2,1,0:T(8,128)S(1)} %bitcast.21, f32[12,80,128]{2,1,0:T(8,128)S(1)} %bitcast.22, f32[12,1,128]{2,1,0:T(1,128)S(1)} %broadcast_in_dim.51.value_ref, f32[12,1,128]{2,1,0:T(1,128)S(1)} %broadcast_in_dim.52.noise_ref, f32[12,128,1]{2,1,0:T(8,128)S(1)} %copy.24.noise_col_ref, ...), custom_call_target="tpu_custom_call" | custom-call | tf_op jit(solution)/shard_map/assimilate/pallas_call | solution.py:398
  217.4 3.0 %copy.27 = f32[80,8,1024]{2,1,0:T(8,128)} copy(f32[80,8,1024]{2,0,1:T(8,128)S(1)} %bitcast.20) | data formatting | bytes 5242880 | tf_op jit(solution)/shard_map/transpose | solution.py:408
  (12 shorter events, 0.1 us)
Async XLA Ops:
  0.0 17.2 %copy-start = (f32[12,8,128]{2,1,0:T(8,128)S(1)}, f32[12,8,128]{2,1,0:T(8,128)}, u32[]{:S(2)}) copy-start(f32[12,8,128]{2,1,0:T(8,128)} %param.11) | copy-start | bytes 147460
  29.5 41.0 %copy-start.1 = (s32[12,24]{1,0:T(8,128)S(1)}, s32[12,24]{1,0:T(8,128)}, u32[]{:S(2)}) copy-start(s32[12,24]{1,0:T(8,128)} %param.12) | copy-start | bytes 3460
where the time goes:
time: 224 us; the launch traced here: 220 us
  Pallas kernels  187 us (83%)
  local copies, waits for them, and re-layouts  24.4 us (11%)
  other arithmetic  8.42 us (4%)
    pallas_call x1, Pallas kernels, body(): call(ensemble.transpose(1, 0, 2), probes, observed[:, None, :], noise[:,...  143 us
    pallas_call x1, Pallas kernels, summed(): pl.pallas_call(functools.partial(sum_kernel, ranks=ranks, rows=rows), out...  31.6 us
    pallas_call x1, Pallas kernels, gathered_table(): pl.pallas_call(functools.partial(table_kernel, ranks=axis_size), out_shap...  13 us
    unnamed x6, local copies, waits for them, and re-layouts  8 us
    gather x1, local copies, waits for them, and re-layouts, portion_of(): picked = jnp.take(ensemble, inside, axis=2)  6.68 us
    reduce_sum x1, other arithmetic, portion_of(): return jnp.sum(picked * (weight * mine[None, :])[None], axis=1)  5.45 us

commit v1 on v0

--- a/solution.py
+++ b/solution.py
@@ -9,7 +9,7 @@
 
 LON_DEV = 16
 CELL_DEV = 1024
-PANEL = 8
+PANEL = 16
 
 highest = lax.Precision.HIGHEST
 f32 = jnp.float32
@@ -33,7 +33,7 @@
     return jnp.exp((e * e + d * d) * (-2.0 / (LON_DEV * LON_DEV)))
 
 
-def eliminate(a_ref, b_ref, noise_root, mem, obs, width):
+def eliminate(a_ref, b_ref, noise_root, mem, obs, width, beside):
     lane = lax.broadcasted_iota(jnp.int32, (1, obs), 1)
     sample = lax.broadcasted_iota(jnp.int32, (1, width), 1) < mem
     for start in range(0, obs, PANEL):
@@ -74,21 +74,23 @@
                 lane < start + PANEL, rows[r] * inverse_root, 0.0
             )
             b_ref[start + r : start + r + 1, :] = solved
+        beside(start // PANEL, obs // PANEL)
         after = start + PANEL
         if after < obs:
-            upper = jnp.concatenate(rows, axis=0)
-            left = upper.T[after:, :]
-            right = jnp.concatenate(
+            u_high, u_low = split(jnp.concatenate(rows, axis=0))
+            high, low = split(jnp.concatenate(
                 [jnp.concatenate(scaled_rows, axis=0), jnp.concatenate(scaled_sides, axis=0)], axis=1
-            )
-            change = jnp.dot(left, right, precision=highest, preferred_element_type=f32)
+            ))
+            upper = jnp.concatenate([u_high.astype(f32), u_high.astype(f32), u_low.astype(f32)], axis=0)
+            left = upper.T.astype(bf16)[after:, :]
+            change = dot(left, jnp.concatenate([high, low, high], axis=0))
             a_ref[after:, :] = jnp.where(in_panel, 0.0, a_ref[after:, :]) - change[:, :obs]
             b_ref[after:, :] = b_ref[after:, :] - change[:, obs:]
 
 
 def kernel_body(
     x_ref, probe_ref, value_ref, noise_ref, noise_col_ref, cell_row_ref, cell_col_ref, list_ref,
-    out_ref, probes, a_ref, b_ref, *, batches, levels, mem, obs, cells, slots, axis_size,
+    out_ref, probes, a_ref, b_ref, weight_ref, left_ref, gains_ref, *, batches, levels, mem, obs, cells, slots, axis_size,
 ):
     tile = lax.axis_index("lon")
     circle = float(LON_DEV * axis_size)
@@ -107,6 +109,19 @@
     lanes = lax.broadcasted_iota(jnp.int32, (obs, obs), 1)
     subs = lax.broadcasted_iota(jnp.int32, (obs, obs), 0)
 
+    def spread_piece(level, start, width):
+        piece = pl.ds(start, width)
+        block = out_ref[level, :, piece]
+        high, low = split(block)
+        crossed = dot(left_ref[...], jnp.concatenate([high, low, high], axis=0))
+        high, low = split(crossed * weight_ref[:, piece])
+        out_ref[level, :, piece] = block + dot(gains_ref[...], jnp.concatenate([high, low, high], axis=0))
+
+    def beside(step, steps):
+        halves = 2 * levels
+        for piece in range(step * halves // steps, (step + 1) * halves // steps):
+            spread_piece(piece // 2, piece % 2 * (cells // 2), cells // 2)
+
     def turn(k, carry):
         now = probes[k]
         centre = jnp.mean(now, axis=0, keepdims=True)
@@ -122,7 +137,7 @@
         b_ref[...] = sides
         root_col = jnp.sqrt(noise_col_ref[k])
         roots = [root_col[j : j + 1, :] for j in range(obs)]
-        eliminate(a_ref, b_ref, roots, mem, obs, obs)
+        eliminate(a_ref, b_ref, roots, mem, obs, obs, beside)
         joined = lax.dot_general(
             a_ref[...], b_ref[...], (((0,), (0,)), ((), ())), precision=highest, preferred_element_type=f32
         )
@@ -196,19 +211,22 @@
         gains_listed = jnp.concatenate([gt_high, gt_high, gt_low, jnp.zeros((obs - 3 * slots, obs), f32)], axis=0)
         gains_listed = gains_listed.T[:mem, : 3 * slots].astype(bf16)
 
-        def spread_level(level, carry, source):
-            block = source[level]
-            high, low = split(block)
-            crossed = dot(left_listed, jnp.concatenate([high, low, high], axis=0))
-            high, low = split(crossed * weight)
-            out_ref[level] = block + dot(gains_listed, jnp.concatenate([high, low, high], axis=0))
-            return carry
-
-        lax.fori_loop(0, levels, functools.partial(spread_level, source=out_ref), 0)
+        weight_ref[...] = weight
+        left_ref[...] = left_listed
+        gains_ref[...] = gains_listed
         return carry
 
     out_ref[...] = x_ref[...]
+    weight_ref[...] = jnp.zeros(weight_ref.shape, f32)
+    left_ref[...] = jnp.zeros(left_ref.shape, bf16)
+    gains_ref[...] = jnp.zeros(gains_ref.shape, bf16)
     lax.fori_loop(0, batches, turn, 0)
+
+    def last(level, carry):
+        spread_piece(level, 0, cells)
+        return carry
+
+    lax.fori_loop(0, levels, last, 0)
 
 
 def peer_of(d, ranks, both):
@@ -391,6 +409,9 @@
             pltpu.VMEM((batches, mem, obs), f32),
             pltpu.VMEM((obs, obs), f32),
             pltpu.VMEM((obs, obs), f32),
+            pltpu.VMEM((slots, cells), f32),
+            pltpu.VMEM((slots, 3 * mem), bf16),
+            pltpu.VMEM((mem, 3 * slots), bf16),
         ],
         compiler_params=pltpu.CompilerParams(vmem_limit_bytes=40 * 1024 * 1024),
         name="assimilate",

time: 224 us -> 169 us (0.75)
  Pallas kernels: 187 us -> 132 us
    pallas_call x1, Pallas kernels: 143 us -> 87.7 us  [body(): call(ensemble.transpose(1, 0, 2), probes, observed[:, None, :], noise[:,...]
where the time goes in v1:
time: 169 us; the launch traced here: 165 us
  Pallas kernels  132 us (78%)
  local copies, waits for them, and re-layouts  24.4 us (14%)
  other arithmetic  8.42 us (5%)
    pallas_call x1, Pallas kernels, body(): call(ensemble.transpose(1, 0, 2), probes, observed[:, None, :], noise[:,...  87.7 us
    pallas_call x1, Pallas kernels, summed(): pl.pallas_call(functools.partial(sum_kernel, ranks=ranks, rows=rows), out...  31.6 us
    pallas_call x1, Pallas kernels, gathered_table(): pl.pallas_call(functools.partial(table_kernel, ranks=axis_size), out_shap...  13 us
    unnamed x6, local copies, waits for them, and re-layouts  8 us
    gather x1, local copies, waits for them, and re-layouts, portion_of(): picked = jnp.take(ensemble, inside, axis=2)  6.68 us
    reduce_sum x1, other arithmetic, portion_of(): return jnp.sum(picked * (weight * mine[None, :])[None], axis=1)  5.45 us

profile of v1, /device:TPU:9, one launch (start us, length us, event | category | flops | bytes accessed | tf_op | source)
XLA Modules:
  0.0 165.3 jit_solution(3250584477954336668)
XLA Ops:
  0.0 0.0 copy-start
  0.0 0.7 compare_select_fusion.2
  0.7 0.7 convert_element_type.17
  1.4 0.8 pad_maximum_fusion
  2.2 0.1 copy.20
  2.2 0.6 pad.12.mine_ref
  2.9 13.0 %table.1 = f32[40,128]{1,0:T(8,128)} custom-call(f32[40,128]{1,0:T(8,128)} %pad.12.mine_ref), custom_call_target="tpu_custom_call" | custom-call | tf_op jit(solution)/shard_map/table/pallas_call | solution.py:333
  15.9 0.8 fusion.3
  16.6 0.6 gather_fusion
  17.2 0.0 copy-done
  17.2 0.6 gather_fusion.2
  17.8 0.3 copy.22
  18.1 4.7 %copy.21 = f32[80,8,1024]{0,1,2:T(8,128)} copy(f32[80,8,1024]{2,1,0:T(8,128)} %param.7) | data formatting | bytes 5242880 | tf_op args[0]
  22.9 6.7 %gather_fusion.1 = f32[1536,80,8]{1,2,0:T(8,128)} fusion(f32[80,8,1024]{0,1,2:T(8,128)} %copy.21, s32[2048]{0:T(1024)S(1)} %pad_clamp_fusion), kind=kCustom, calls=%fused_computation.1 | custom fusion | bytes 7870464 | tf_op jit(solution)/shard_map/vmap(jit(_take))/gather | solution.py:393
  29.5 0.0 copy-start.1
  29.5 5.4 %fusion = f32[12,80,128]{1,2,0:T(8,128)S(1)} fusion(f32[12,128,80,8]{2,3,1,0:T(8,128)} %bitcast.23, f32[12,8,128]{1,2,0:T(8,128)S(1)} %copy.22, pred[12,128]{1,0:T(8,128)(4,1)S(1)} %get-tuple-element.8), kind=kLoop, calls=%fused_computation.7 | loop fusion | flops 2826240 | bytes 4474368 | tf_op jit(solution)/shard_map/vmap()/reduce_sum | solution.py:394
  35.0 0.3 copy.23
  35.2 0.8 pad.13.mine_ref
  36.1 31.6 %total.1 = f32[1024,128]{1,0:T(8,128)} custom-call(f32[1024,128]{1,0:T(8,128)} %pad.13.mine_ref), custom_call_target="tpu_custom_call" | custom-call | tf_op jit(solution)/shard_map/total/pallas_call | solution.py:352
  67.7 1.1 slice.17
  68.8 0.3 copy.25.cell_col_ref
  69.1 0.6 gather_fusion.4
  69.7 0.3 copy.24.noise_col_ref
  70.0 0.6 gather_fusion.3
  70.5 0.0 copy-done.1
  70.6 0.6 gather_fusion.5
  71.1 0.2 copy.26.list_ref
  71.3 3.3 %copy.29 = f32[80,8,1024]{2,0,1:T(8,128)S(1)} copy(f32[80,8,1024]{2,1,0:T(8,128)} %param.7) | data formatting | bytes 5242880 | tf_op args[0]
  74.5 87.7 %assimilate.1 = f32[8,80,1024]{2,1,0:T(8,128)S(1)} custom-call(f32[8,80,1024]{2,1,0:T(8,128)S(1)} %bitcast.21, f32[12,80,128]{2,1,0:T(8,128)S(1)} %bitcast.22, f32[12,1,128]{2,1,0:T(1,128)S(1)} %broadcast_in_dim.51.value_ref, f32[12,1,128]{2,1,0:T(1,128)S(1)} %broadcast_in_dim.52.noise_ref, f32[12,128,1]{2,1,0:T(8,128)S(1)} %copy.24.noise_col_ref, ...), custom_call_target="tpu_custom_call" | custom-call | tf_op jit(solution)/shard_map/assimilate/pallas_call | solution.py:419
  162.3 3.0 %copy.27 = f32[80,8,1024]{2,1,0:T(8,128)} copy(f32[80,8,1024]{2,0,1:T(8,128)S(1)} %bitcast.20) | data formatting | bytes 5242880 | tf_op jit(solution)/shard_map/transpose | solution.py:429
  (12 shorter events, 0.1 us)
Async XLA Ops:
  0.0 17.2 %copy-start = (f32[12,8,128]{2,1,0:T(8,128)S(1)}, f32[12,8,128]{2,1,0:T(8,128)}, u32[]{:S(2)}) copy-start(f32[12,8,128]{2,1,0:T(8,128)} %param.11) | copy-start | bytes 147460
  29.5 41.0 %copy-start.1 = (s32[12,24]{1,0:T(8,128)S(1)}, s32[12,24]{1,0:T(8,128)}, u32[]{:S(2)}) copy-start(s32[12,24]{1,0:T(8,128)} %param.12) | copy-start | bytes 3460

commit v2 on v1

v2 whole, which is shorter than its diff:
```python
import functools

import jax
import jax.numpy as jnp
from jax import lax
from jax.experimental import pallas as pl
from jax.experimental.pallas import tpu as pltpu
from jax.sharding import PartitionSpec as P

LON_DEV = 16
CELL_DEV = 1024
PANEL = 16

highest = lax.Precision.HIGHEST
f32 = jnp.float32
bf16 = jnp.bfloat16


def split(x):
    high = x.astype(bf16)
    low = (x - high.astype(f32)).astype(bf16)
    return high, low


def dot(a, b):
    return jnp.dot(a, b, preferred_element_type=f32)


def tapered_weight(row_a, col_a, row_c, col_c, circle):
    e = jnp.abs(col_a - col_c)
    e = jnp.minimum(e, circle - e)
    d = row_a - row_c
    return jnp.exp((e * e + d * d) * (-2.0 / (LON_DEV * LON_DEV)))


def eliminate(a_ref, b_ref, noise_root, mem, obs, width, beside):
    lane = lax.broadcasted_iota(jnp.int32, (1, obs), 1)
    sample = lax.broadcasted_iota(jnp.int32, (1, width), 1) < mem
    for start in range(0, obs, PANEL):
        spot = [[None] * PANEL for _ in range(PANEL)]
        for i in range(PANEL):
            for s in range(i + 1):
                spot[i][s] = jnp.broadcast_to(
                    a_ref[start + i : start + i + 1, start + s : start + s + 1], (1, obs)
                )
        in_panel = (lane >= start) & (lane < start + PANEL)
        rows = []
        sides = []
        for i in range(PANEL):
            row = a_ref[start + i : start + i + 1, :]
            rows.append(jnp.where(in_panel, jnp.where(lane == start + i, 1.0, 0.0), row))
            sides.append(b_ref[start + i : start + i + 1, :])
        scaled_rows = []
        scaled_sides = []
        for r in range(PANEL):
            pivot = spot[r][r]
            inverse_root = lax.rsqrt(pivot)
            inverse = inverse_root * inverse_root
            root = pivot * inverse_root
            added = jnp.where(sample, noise_root[start + r], 0.0)
            factor = 1.0 / (root + added)
            below = [spot[i][r] * inverse for i in range(r + 1, PANEL)]
            for n, i in enumerate(range(r + 1, PANEL)):
                for s in range(r + 1, i + 1):
                    spot[i][s] = spot[i][s] - below[n] * spot[s][r]
            solved = sides[r] * factor
            passing = solved * root
            for n, i in enumerate(range(r + 1, PANEL)):
                rows[i] = rows[i] - below[n] * rows[r]
                sides[i] = sides[i] - below[n] * passing
            scaled_rows.append(rows[r] * inverse)
            scaled_sides.append(solved * inverse_root)
            a_ref[start + r : start + r + 1, :] = jnp.where(
                lane < start + PANEL, rows[r] * inverse_root, 0.0
            )
            b_ref[start + r : start + r + 1, :] = solved
        beside(start // PANEL, obs // PANEL)
        after = start + PANEL
        if after < obs:
            u_high, u_low = split(jnp.concatenate(rows, axis=0))
            high, low = split(jnp.concatenate(
                [jnp.concatenate(scaled_rows, axis=0), jnp.concatenate(scaled_sides, axis=0)], axis=1
            ))
            upper = jnp.concatenate([u_high.astype(f32), u_high.astype(f32), u_low.astype(f32)], axis=0)
            left = upper.T.astype(bf16)[after:, :]
            change = dot(left, jnp.concatenate([high, low, high], axis=0))
            a_ref[after:, :] = jnp.where(in_panel, 0.0, a_ref[after:, :]) - change[:, :obs]
            b_ref[after:, :] = b_ref[after:, :] - change[:, obs:]


def kernel_body(
    order_ref, x_ref, landed_ref, table_ref, list_ref, out_ref,
    state, natural, probes, a_ref, b_ref, weight_ref, left_ref, gains_ref, rows_ref, noise_cols, cell_cols,
    list_cols, sem_in, sem_out, *, batches, levels, mem, obs, cells, slots, axis_size, own_max,
):
    def fetch(level):
        return pltpu.make_async_copy(x_ref.at[:, level, :], state.at[level], sem_in.at[level])

    def deliver(level):
        return pltpu.make_async_copy(state.at[level], out_ref.at[:, level, :], sem_out.at[level])

    for level in range(levels):
        fetch(level).start()
    tile = lax.axis_index("lon")
    circle = float(LON_DEV * axis_size)
    scale = 1.0 / (mem - 1)
    cell = lax.broadcasted_iota(jnp.int32, (1, cells), 1)
    here_row = (cell // LON_DEV).astype(f32)
    here_col = (tile * LON_DEV + cell % LON_DEV).astype(f32)
    lanes = lax.broadcasted_iota(jnp.int32, (obs, obs), 1)
    subs = lax.broadcasted_iota(jnp.int32, (obs, obs), 0)
    table = table_ref[...]
    rows = table.T
    rows_ref[...] = rows
    count = axis_size * own_max
    spot = lax.broadcasted_iota(jnp.int32, (count, obs), 0).astype(f32)
    listed_rows = jnp.concatenate(
        [list_ref[...].astype(f32), jnp.full((batches, obs - list_ref.shape[1]), float(obs), f32)], axis=1
    )
    listed_rows = jnp.concatenate([listed_rows, jnp.zeros((obs - batches, obs), f32)], axis=0).T
    parts = landed_ref.shape[1]
    share = -(-batches // parts)
    for b in range(batches):
        cell_row = rows[b : b + 1, :].astype(jnp.int32)
        tile_row = cell_row // CELL_DEV
        cell_col = jnp.broadcast_to(table[:, b : b + 1], (obs, obs))
        tile_col = cell_col.astype(jnp.int32) // CELL_DEV
        earlier = (tile_col == tile_row) & (subs < lanes)
        rank = jnp.sum(jnp.where(earlier, 1.0, 0.0), axis=0, keepdims=True)
        slot = tile_row.astype(f32) * own_max + rank
        found = jnp.where(spot == slot, 1.0, 0.0).astype(bf16)
        first = b % share * mem
        slab = landed_ref[:, b // share, :, first : first + mem].reshape(count, mem)
        high, low = split(slab)
        left = jnp.concatenate([high.astype(f32), low.astype(f32)], axis=0).T.astype(bf16)
        natural[b] = dot(left, jnp.concatenate([found, found], axis=0))
        noise_cols[b] = jnp.sqrt(jnp.broadcast_to(table[:, 2 * batches + b : 2 * batches + b + 1], (obs, obs)))
        cell_cols[b] = cell_col
        list_cols[b] = jnp.broadcast_to(listed_rows[:slots, b : b + 1], (slots, obs))

    def arrange(k, carry):
        probes[k] = natural[order_ref[k]]
        return carry

    lax.fori_loop(0, batches, arrange, 0)

    def place_of(cells_now):
        cells_now = cells_now.astype(jnp.int32)
        its_tile = cells_now // CELL_DEV
        within = cells_now - its_tile * CELL_DEV
        row = within // LON_DEV
        col = its_tile * LON_DEV + within - row * LON_DEV
        return row.astype(f32), col.astype(f32), its_tile.astype(f32)

    def spread_piece(level, start, width):
        piece = pl.ds(start, width)
        block = state[level, :, piece]
        high, low = split(block)
        crossed = dot(left_ref[...], jnp.concatenate([high, low, high], axis=0))
        high, low = split(crossed * weight_ref[:, piece])
        state[level, :, piece] = block + dot(gains_ref[...], jnp.concatenate([high, low, high], axis=0))

    def beside(step, steps):
        halves = 2 * levels
        for piece in range(step * halves // steps, (step + 1) * halves // steps):
            spread_piece(piece // 2, piece % 2 * (cells // 2), cells // 2)

    def turn(k, carry):
        block = order_ref[k]
        now = probes[k]
        centre = jnp.mean(now, axis=0, keepdims=True)
        spread = now - centre
        innovation = rows_ref[pl.ds(batches + block, 1), :] - centre
        padded = jnp.concatenate(
            [spread, innovation, jnp.zeros((obs - mem - 1, obs), f32)], axis=0
        )
        sides = padded.T
        noise_row = rows_ref[pl.ds(2 * batches + block, 1), :]
        covariance = jnp.dot(sides[:, :mem], spread, precision=highest, preferred_element_type=f32) * scale
        a_ref[...] = covariance + jnp.where(lanes == subs, noise_row, 0.0)
        b_ref[...] = sides
        root_col = noise_cols[block]
        roots = [root_col[j : j + 1, :] for j in range(obs)]
        eliminate(a_ref, b_ref, roots, mem, obs, obs, beside)
        joined = lax.dot_general(
            a_ref[...], b_ref[...], (((0,), (0,)), ((), ())), precision=highest, preferred_element_type=f32
        )
        gain_t = joined[:, mem : mem + 1] - joined
        gain = gain_t.T[:mem, :]

        s_high, s_low = split(spread)
        stacked = jnp.concatenate([s_high.astype(f32), s_high.astype(f32), s_low.astype(f32)], axis=0)
        left = stacked.T.astype(bf16)
        g_high, g_low = split(gain)
        gains = jnp.concatenate([g_high, g_high, g_low], axis=1)

        from_row, from_col, from_tile = place_of(cell_cols[block])

        def renew(b, carry):
            @pl.when(2 * b + 1 > k)
            def _():
                upcoming = jnp.concatenate([probes[2 * b], probes[2 * b + 1]], axis=1)
                high, low = split(upcoming)
                crossed = dot(left, jnp.concatenate([high, low, high], axis=0))
                weights = []
                for u in range(2):
                    target_row, target_col, target_tile = place_of(
                        rows_ref[pl.ds(order_ref[2 * b + u], 1), :]
                    )
                    weight = tapered_weight(from_row, from_col, target_row, target_col, circle)
                    apart = jnp.abs(from_tile - target_tile)
                    near = (apart < 1.5) | (apart > axis_size - 1.5)
                    weights.append(jnp.where(near, weight * scale, 0.0))
                tapered = crossed * jnp.concatenate(weights, axis=1)
                high, low = split(tapered)
                upcoming = upcoming + dot(gains, jnp.concatenate([high, low, high], axis=0))
                probes[2 * b] = upcoming[:, :obs]
                probes[2 * b + 1] = upcoming[:, obs:]

            return carry

        for b in range(batches // 2):
            renew(b, 0)

        listed = list_cols[block]
        chosen = lanes[:slots].astype(f32) == listed
        select = chosen.astype(bf16)
        pick_row, pick_col, _ = place_of(rows_ref[pl.ds(block, 1), :])
        list_row = jnp.sum(jnp.where(chosen, pick_row, 0.0), axis=1, keepdims=True)
        list_col = jnp.sum(jnp.where(chosen, pick_col, 0.0), axis=1, keepdims=True)
        usable = jnp.where(listed[:, :1] < obs, scale, 0.0)
        weight = tapered_weight(list_row, list_col, here_row, here_col, circle) * usable
        left_listed = dot(select, left).astype(bf16)
        gt_high, gt_low = split(gain_t)
        gt_high = dot(select, gt_high)
        gt_low = dot(select, gt_low)
        gains_listed = jnp.concatenate([gt_high, gt_high, gt_low, jnp.zeros((obs - 3 * slots, obs), f32)], axis=0)
        gains_listed = gains_listed.T[:mem, : 3 * slots].astype(bf16)

        weight_ref[...] = weight
        left_ref[...] = left_listed
        gains_ref[...] = gains_listed
        return carry

    weight_ref[...] = jnp.zeros(weight_ref.shape, f32)
    left_ref[...] = jnp.zeros(left_ref.shape, bf16)
    gains_ref[...] = jnp.zeros(gains_ref.shape, bf16)
    for level in range(levels):
        fetch(level).wait()
    lax.fori_loop(0, batches, turn, 0)

    def last(level, carry):
        spread_piece(level, 0, cells)
        deliver(level).start()
        return carry

    lax.fori_loop(0, levels, last, 0)
    for level in range(levels):
        deliver(level).wait()


def gather_kernel(
    x_ref, cell_ref, value_ref, noise_ref, weight_ref, landed, table_ref,
    x_in, mine, tables, packed, partial, total, x_sem,
    table_send, table_recv, pair_send, pair_recv, send_sem, recv_sem, pass_send, pass_recv,
    *, ranks, cores, batches, mem, levels, cells, obs, own_max,
):
    lon, lev = lax.axis_index("lon"), lax.axis_index("lev")
    mesh_id = pl.DeviceIdType.MESH
    fetch = pltpu.make_async_copy(x_ref, x_in, x_sem)
    fetch.start()
    own = cell_ref.shape[0]
    depth = mine.shape[0]
    row = jnp.concatenate(
        [cell_ref[...].astype(f32), value_ref[...], noise_ref[...], jnp.zeros((own, 128 - 3 * batches), f32)], axis=1
    )
    if own < depth:
        row = jnp.concatenate([row, jnp.zeros((depth - own, 128), f32)], axis=0)
    mine[...] = row

    def chip(d):
        return lax.rem(lon + d, ranks), lev

    def core(d):
        return lon, lax.rem(lev + d, cores)

    barrier = pltpu.get_barrier_semaphore()

    def announce(d, carry):
        pl.semaphore_signal(barrier, inc=1, device_id=chip(d), device_id_type=mesh_id)
        return carry

    lax.fori_loop(1, ranks, announce, 0)
    for d in range(1, cores):
        pl.semaphore_signal(barrier, inc=1, device_id=core(d), device_id_type=mesh_id)
    pl.semaphore_wait(barrier, ranks + cores - 2)

    def table_to(d):
        return pltpu.make_async_remote_copy(
            src_ref=mine, dst_ref=tables.at[lon], send_sem=table_send.at[d], recv_sem=table_recv.at[d],
            device_id=chip(d), device_id_type=mesh_id,
        )

    def start_table(d, carry):
        table_to(d).start()
        return carry

    def wait_table(d, carry):
        table_to(d).wait()
        return carry

    lax.fori_loop(1, ranks, start_table, 0)
    tables[lon] = row
    lax.fori_loop(1, ranks, wait_table, 0)
    if own == depth:
        table = tables[...].reshape(obs, 128)
    else:
        table = jnp.concatenate([tables[t, :own, :] for t in range(ranks)], axis=0)
    table_ref[...] = table

    lane = lax.broadcasted_iota(jnp.int32, (obs, 128), 1)
    sub = lax.broadcasted_iota(jnp.int32, (obs, 128), 0)
    cell = jnp.where(lane < batches, table, -1.0).astype(jnp.int32)
    within = cell - lon * cells
    owned = (within >= 0) & (within < cells)
    before = jnp.where(lax.broadcasted_iota(jnp.int32, (obs, obs), 1) < lax.broadcasted_iota(jnp.int32, (obs, obs), 0), 1.0, 0.0)
    rank = dot(before.astype(bf16), jnp.where(owned, 1.0, 0.0).astype(bf16))
    code = jnp.where(owned, rank, -1.0)
    within = jnp.where(owned, within, 0)
    upper = within // LON_DEV
    lower = within - upper * LON_DEV
    deep = lax.broadcasted_iota(jnp.int32, (128, 128), 0)
    wide = lax.broadcasted_iota(jnp.int32, (128, 128), 1)
    spread_out = jnp.where((wide // own_max == deep) & (deep < batches), 1.0, 0.0).astype(bf16)
    wide_code = dot(code.astype(bf16), spread_out)
    wide_upper = dot(upper.astype(f32).astype(bf16), spread_out)
    wide_lower = dot(lower.astype(f32).astype(bf16), spread_out)
    slot = (lane - lane // own_max * own_max).astype(f32)
    taken = (wide_code == slot) & (lane < batches * own_max)
    chosen = jnp.where(taken, 1.0, 0.0)
    column = jnp.sum(jnp.where(taken, wide_upper * LON_DEV + wide_lower, 0.0), axis=0, keepdims=True)
    weighed = jnp.dot(
        weight_ref[...].reshape(batches * levels, obs), chosen, precision=highest, preferred_element_type=f32
    )
    block_of = lax.broadcasted_iota(jnp.int32, (levels, 128), 1) // own_max
    weight = jnp.zeros((levels, 128), f32)
    for b in range(batches):
        weight = jnp.where(block_of == b, weighed[b * levels : (b + 1) * levels, :], weight)
    at = lax.broadcasted_iota(jnp.int32, (cells, 128), 0).astype(f32)
    hot = jnp.where(at == column, 1.0, 0.0).astype(bf16)
    fetch.wait()
    pieces = []
    group = 16
    for m in range(0, mem, group):
        part = x_in[m : m + group].reshape(group * levels, cells)
        high, low = split(part)
        picked = (dot(high, hot) + dot(low, hot)).reshape(group, levels, 128)
        pieces.append(jnp.sum(picked * weight[None], axis=1))
    portion = jnp.concatenate(pieces + [jnp.zeros((128 - mem, 128), f32)], axis=0).T
    share = -(-batches // cores)
    width = packed.shape[2]
    for h in range(cores):
        line = [portion[b * own_max : (b + 1) * own_max, :mem] for b in range(h * share, min((h + 1) * share, batches))]
        gap = width - len(line) * mem
        if gap:
            line.append(jnp.zeros((own_max, gap), f32))
        packed[h] = jnp.concatenate(line, axis=1)

    def pair_to(d):
        return pltpu.make_async_remote_copy(
            src_ref=packed.at[lax.rem(lev + d, cores)], dst_ref=partial.at[d], send_sem=pair_send.at[d],
            recv_sem=pair_recv.at[d], device_id=core(d), device_id_type=mesh_id,
        )

    for d in range(1, cores):
        pair_to(d).start()
    sum_now = packed[lev]
    for d in range(1, cores):
        pair_to(d).wait()
        sum_now = sum_now + partial[d]
    total[...] = sum_now

    def send_to(d):
        return pltpu.make_async_remote_copy(
            src_ref=total, dst_ref=landed.at[lon, lev], send_sem=send_sem.at[d], recv_sem=recv_sem.at[d],
            device_id=chip(d), device_id_type=mesh_id,
        )

    def give_to(d):
        return pltpu.make_async_remote_copy(
            src_ref=total, dst_ref=landed.at[lon, lev], send_sem=pass_send.at[d, 0], recv_sem=pass_recv.at[d, 0],
            device_id=core(d), device_id_type=mesh_id,
        )

    def pass_on(d, e):
        source = lax.rem(lon - d + ranks, ranks)
        return pltpu.make_async_remote_copy(
            src_ref=landed.at[source, lev], dst_ref=landed.at[source, lev], send_sem=pass_send.at[e, d],
            recv_sem=pass_recv.at[e, d], device_id=core(e), device_id_type=mesh_id,
        )

    def start_send(d, carry):
        send_to(d).start()
        return carry

    def relay(d, carry):
        send_to(d).wait()
        for e in range(1, cores):
            pass_on(d, e).start()
        return carry

    def wait_relay(d, carry):
        for e in range(1, cores):
            pass_on(d, e).wait()
        return carry

    lax.fori_loop(1, ranks, start_send, 0)
    for d in range(1, cores):
        give_to(d).start()
    landed[lon, lev] = sum_now
    lax.fori_loop(1, ranks, relay, 0)
    for d in range(1, cores):
        give_to(d).wait()
    lax.fori_loop(1, ranks, wait_relay, 0)


def body(ensemble, obs_cell, obs_value, obs_noise, obs_weight, tile_lists, batch_order):
    mem, levels, cells = ensemble.shape
    batches, own = obs_cell.shape
    ranks, cores = lax.axis_size("lon"), lax.axis_size("lev")
    obs = own * ranks
    own_max = 8
    slots = -(-tile_lists.shape[1] // 16) * 16
    width = -(-(-(-batches // cores) * mem) // 128) * 128
    depth = -(-own // 8) * 8
    vmem = pl.BlockSpec(memory_space=pltpu.VMEM)
    hbm = pl.BlockSpec(memory_space=pl.ANY)
    dma = pltpu.SemaphoreType.DMA
    landed, table = pl.pallas_call(
        functools.partial(
            gather_kernel, ranks=ranks, cores=cores, batches=batches, mem=mem, levels=levels, cells=cells,
            obs=obs, own_max=own_max,
        ),
        out_shape=[
            jax.ShapeDtypeStruct((ranks, cores, own_max, width), f32), jax.ShapeDtypeStruct((obs, 128), f32)
        ],
        in_specs=[hbm] + [vmem] * 4,
        out_specs=[vmem, vmem],
        scratch_shapes=[
            pltpu.VMEM((mem, levels, cells), f32),
            pltpu.VMEM((depth, 128), f32),
            pltpu.VMEM((ranks, depth, 128), f32),
            pltpu.VMEM((cores, own_max, width), f32),
            pltpu.VMEM((cores, own_max, width), f32),
            pltpu.VMEM((own_max, width), f32),
            dma(()), dma((ranks,)), dma((ranks,)), dma((cores,)), dma((cores,)), dma((ranks,)), dma((ranks,)),
            dma((cores, ranks)), dma((cores, ranks)),
        ],
        compiler_params=pltpu.CompilerParams(
            collective_id=0, has_side_effects=True, vmem_limit_bytes=40 * 1024 * 1024
        ),
        name="gather",
    )(ensemble, obs_cell.T, obs_value.T, obs_noise.T, obs_weight)

    return pl.pallas_call(
        functools.partial(
            kernel_body, batches=batches, levels=levels, mem=mem, obs=obs, cells=cells, slots=slots,
            axis_size=ranks, own_max=own_max,
        ),
        out_shape=jax.ShapeDtypeStruct((mem, levels, cells), f32),
        in_specs=[pl.BlockSpec(memory_space=pltpu.SMEM), hbm, vmem, vmem, vmem],
        out_specs=hbm,
        scratch_shapes=[
            pltpu.VMEM((levels, mem, cells), f32),
            pltpu.VMEM((batches, mem, obs), f32),
            pltpu.VMEM((batches, mem, obs), f32),
            pltpu.VMEM((obs, obs), f32),
            pltpu.VMEM((obs, obs), f32),
            pltpu.VMEM((slots, cells), f32),
            pltpu.VMEM((slots, 3 * mem), bf16),
            pltpu.VMEM((mem, 3 * slots), bf16),
            pltpu.VMEM((128, obs), f32),
            pltpu.VMEM((batches, obs, obs), f32),
            pltpu.VMEM((batches, obs, obs), f32),
            pltpu.VMEM((batches, slots, obs), f32),
            dma((levels,)),
            dma((levels,)),
        ],
        compiler_params=pltpu.CompilerParams(vmem_limit_bytes=40 * 1024 * 1024),
        name="assimilate",
    )(batch_order, ensemble, landed, table, tile_lists)


def solution(mesh):
    return jax.shard_map(
        body,
        mesh=mesh,
        in_specs=(
            P(None, "lev", "lon"),
            P(None, "lon"),
            P(None, "lon"),
            P(None, "lon"),
            P(None, "lev", None),
            P(None, "lon"),
            P(),
        ),
        out_specs=P(None, "lev", "lon"),
        check_vma=False,
    )
```

time: 169 us -> 118 us (0.70); the launches traced: 165 us -> 118 us
  local copies, waits for them, and re-layouts: 24.4 us -> 4.62 us
  Pallas kernels: 132 us -> 113 us
  other arithmetic: 8.42 us -> 0 us
    pallas_call x3 -> x2, Pallas kernels: 132 us -> 113 us  [the longest x1 90.8 us: body(): pl.pallas_call(functools.partial(kernel_body, batches=batches, levels=lev...]
    gather x8 -> x0, local copies, waits for them, and re-layouts: 9.77 us -> none  [the longest x1 6.68 us: portion_of(): picked = jnp.take(ensemble, inside, axis=2)]
    reduce_sum x1 -> x0, other arithmetic: 5.45 us -> none  [portion_of(): return jnp.sum(picked * (weight * mine[None, :])[None], axis=1)]
    unnamed x6 -> x14, local copies, waits for them, and re-layouts: 8 us -> 4.62 us
    transpose x1 -> x0, local copies, waits for them, and re-layouts: 3.01 us -> none  [body(): return out.transpose(1, 0, 2)]
where the time goes in v2:
time: 118 us
  Pallas kernels  113 us (96%)
  local copies, waits for them, and re-layouts  4.62 us (4%)
    pallas_call x1, Pallas kernels, body(): pl.pallas_call(functools.partial(kernel_body, batches=batches, levels=lev...  90.8 us
    pallas_call x1, Pallas kernels, body(): pl.pallas_call(functools.partial(gather_kernel, ranks=ranks, cores=cores,...  22.5 us
    unnamed x14, local copies, waits for them, and re-layouts  4.62 us

profile of v2, /device:TPU:9, one launch (start us, length us, event | category | flops | bytes accessed | tf_op | source)
XLA Modules:
  0.0 118.0 jit_solution(10418829265924275279)
XLA Ops:
  0.0 0.0 copy-start.6
  0.0 0.0 copy-start
  0.0 1.8 %copy-done = f32[80,8,1024]{2,1,0:T(8,128)S(1)} copy-done((f32[80,8,1024]{2,1,0:T(8,128)S(1)}, f32[80,8,1024]{2,1,0:T(8,128)}, u32[]{:S(2)}) %copy-start) | copy-done | bytes 2621464
  1.8 0.0 copy-start.1
  1.8 0.8 copy-done.1
  2.6 0.0 copy-start.3
  2.6 0.7 copy-done.3
  3.2 0.0 copy-start.4
  3.2 0.7 copy-done.4
  3.9 0.0 copy-start.5
  3.9 0.7 copy-done.5
  4.6 0.0 copy-start.2
  4.6 22.5 %gather.1 = (f32[16,2,8,512]{3,2,1,0:T(8,128)S(1)}, f32[128,128]{1,0:T(8,128)S(1)}) custom-call(f32[80,8,1024]{2,1,0:T(8,128)S(1)} %copy-done, s32[8,12]{1,0:T(8,128)S(1)} %bitcast.3, f32[8,12]{1,0:T(8,128)S(1)} %bitcast.4, f32[8,12]{1,0:T(8,128)S(1)} %bitcast.5, f32[12,8,128]{2,1,0:T(8,128)S(1)} %copy-done.1), custom_call_target="tpu_custom_call" | custom-call | tf_op jit(solution)/shard_map/gather/pallas_call | solution.py:439
  27.2 0.0 copy-done.6
  27.2 0.0 copy-done.2
  27.2 90.8 %assimilate.1 = f32[80,8,1024]{2,1,0:T(8,128)} custom-call(s32[12]{0:T(128)S(1)} %copy-done.6, f32[80,8,1024]{2,1,0:T(8,128)S(1)} %copy-done, f32[16,2,8,512]{3,2,1,0:T(8,128)S(1)} %get-tuple-element.7.landed_ref, f32[128,128]{1,0:T(8,128)S(1)} %get-tuple-element.8.table_ref, s32[12,24]{1,0:T(8,128)S(1)} %copy-done.2), custom_call_target="tpu_custom_call" | custom-call | tf_op jit(solution)/shard_map/assimilate/pallas_call | solution.py:465
Async XLA Ops:
  0.0 27.2 %copy-start.6 = (s32[12]{0:T(128)S(1)}, s32[12]{0:T(128)}, u32[]{:S(2)}) copy-start(s32[12]{0:T(128)} %order_ref.1) | copy-start | bytes 148
  0.0 1.8 %copy-start = (f32[80,8,1024]{2,1,0:T(8,128)S(1)}, f32[80,8,1024]{2,1,0:T(8,128)}, u32[]{:S(2)}) copy-start(f32[80,8,1024]{2,1,0:T(8,128)} %x_ref.3) | copy-start | bytes 7864324
  1.8 0.8 copy-start.1
  2.6 0.7 copy-start.3
  3.2 0.7 copy-start.4
  3.9 0.7 copy-start.5
  4.6 22.6 %copy-start.2 = (s32[12,24]{1,0:T(8,128)S(1)}, s32[12,24]{1,0:T(8,128)}, u32[]{:S(2)}) copy-start(s32[12,24]{1,0:T(8,128)} %list_ref.1) | copy-start | bytes 3460

commit v3 on v2

--- a/solution.py
+++ b/solution.py
@@ -10,6 +10,7 @@
 LON_DEV = 16
 CELL_DEV = 1024
 PANEL = 16
+GROUP = 2
 
 highest = lax.Precision.HIGHEST
 f32 = jnp.float32
@@ -89,9 +90,9 @@
 
 
 def kernel_body(
-    order_ref, x_ref, landed_ref, table_ref, list_ref, out_ref,
+    order_ref, x_ref, landed_ref, table_ref, list_hbm, out_ref,
     state, natural, probes, a_ref, b_ref, weight_ref, left_ref, gains_ref, rows_ref, noise_cols, cell_cols,
-    list_cols, sem_in, sem_out, *, batches, levels, mem, obs, cells, slots, axis_size, own_max,
+    list_cols, list_ref, sem_list, sem_in, sem_out, *, batches, levels, mem, obs, cells, slots, axis_size, own_max,
 ):
     def fetch(level):
         return pltpu.make_async_copy(x_ref.at[:, level, :], state.at[level], sem_in.at[level])
@@ -99,6 +100,8 @@
     def deliver(level):
         return pltpu.make_async_copy(state.at[level], out_ref.at[:, level, :], sem_out.at[level])
 
+    list_copy = pltpu.make_async_copy(list_hbm, list_ref, sem_list)
+    list_copy.start()
     for level in range(levels):
         fetch(level).start()
     tile = lax.axis_index("lon")
@@ -114,28 +117,31 @@
     rows_ref[...] = rows
     count = axis_size * own_max
     spot = lax.broadcasted_iota(jnp.int32, (count, obs), 0).astype(f32)
+    list_copy.wait()
     listed_rows = jnp.concatenate(
         [list_ref[...].astype(f32), jnp.full((batches, obs - list_ref.shape[1]), float(obs), f32)], axis=1
     )
     listed_rows = jnp.concatenate([listed_rows, jnp.zeros((obs - batches, obs), f32)], axis=0).T
     parts = landed_ref.shape[1]
     share = -(-batches // parts)
+    lane_b = lanes[:, :128]
+    tile_cols = (jnp.where(lane_b < batches, table, 0.0).astype(jnp.int32) // CELL_DEV).astype(f32)
+    tile_rows = tile_cols.T
+    roots_all = jnp.sqrt(jnp.where((lane_b >= 2 * batches) & (lane_b < 3 * batches), table, 1.0))
+    sooner = jnp.where(subs < lanes, 1.0, 0.0)
     for b in range(batches):
-        cell_row = rows[b : b + 1, :].astype(jnp.int32)
-        tile_row = cell_row // CELL_DEV
-        cell_col = jnp.broadcast_to(table[:, b : b + 1], (obs, obs))
-        tile_col = cell_col.astype(jnp.int32) // CELL_DEV
-        earlier = (tile_col == tile_row) & (subs < lanes)
-        rank = jnp.sum(jnp.where(earlier, 1.0, 0.0), axis=0, keepdims=True)
-        slot = tile_row.astype(f32) * own_max + rank
+        tile_row = tile_rows[b : b + 1, :]
+        tile_col = jnp.broadcast_to(tile_cols[:, b : b + 1], (obs, obs))
+        rank = jnp.sum(jnp.where(tile_col == tile_row, sooner, 0.0), axis=0, keepdims=True)
+        slot = tile_row * own_max + rank
         found = jnp.where(spot == slot, 1.0, 0.0).astype(bf16)
         first = b % share * mem
         slab = landed_ref[:, b // share, :, first : first + mem].reshape(count, mem)
         high, low = split(slab)
         left = jnp.concatenate([high.astype(f32), low.astype(f32)], axis=0).T.astype(bf16)
         natural[b] = dot(left, jnp.concatenate([found, found], axis=0))
-        noise_cols[b] = jnp.sqrt(jnp.broadcast_to(table[:, 2 * batches + b : 2 * batches + b + 1], (obs, obs)))
-        cell_cols[b] = cell_col
+        noise_cols[b] = jnp.broadcast_to(roots_all[:, 2 * batches + b : 2 * batches + b + 1], (obs, obs))
+        cell_cols[b] = jnp.broadcast_to(table[:, b : b + 1], (obs, obs))
         list_cols[b] = jnp.broadcast_to(listed_rows[:slots, b : b + 1], (slots, obs))
 
     def arrange(k, carry):
@@ -176,51 +182,49 @@
         )
         sides = padded.T
         noise_row = rows_ref[pl.ds(2 * batches + block, 1), :]
-        covariance = jnp.dot(sides[:, :mem], spread, precision=highest, preferred_element_type=f32) * scale
+        s_high, s_low = split(spread)
+        stacked = jnp.concatenate([s_high.astype(f32), s_high.astype(f32), s_low.astype(f32)], axis=0)
+        left = stacked.T.astype(bf16)
+        covariance = dot(left, jnp.concatenate([s_high, s_low, s_high], axis=0)) * scale
         a_ref[...] = covariance + jnp.where(lanes == subs, noise_row, 0.0)
         b_ref[...] = sides
         root_col = noise_cols[block]
         roots = [root_col[j : j + 1, :] for j in range(obs)]
         eliminate(a_ref, b_ref, roots, mem, obs, obs, beside)
-        joined = lax.dot_general(
-            a_ref[...], b_ref[...], (((0,), (0,)), ((), ())), precision=highest, preferred_element_type=f32
+        f_high, f_low = split(a_ref[...].T)
+        b_high, b_low = split(b_ref[...])
+        joined = dot(
+            jnp.concatenate([f_high, f_high, f_low], axis=1), jnp.concatenate([b_high, b_low, b_high], axis=0)
         )
         gain_t = joined[:, mem : mem + 1] - joined
         gain = gain_t.T[:mem, :]
 
-        s_high, s_low = split(spread)
-        stacked = jnp.concatenate([s_high.astype(f32), s_high.astype(f32), s_low.astype(f32)], axis=0)
-        left = stacked.T.astype(bf16)
         g_high, g_low = split(gain)
         gains = jnp.concatenate([g_high, g_high, g_low], axis=1)
 
         from_row, from_col, from_tile = place_of(cell_cols[block])
 
-        def renew(b, carry):
-            @pl.when(2 * b + 1 > k)
+        def renew(first):
+            @pl.when(first + GROUP - 1 > k)
             def _():
-                upcoming = jnp.concatenate([probes[2 * b], probes[2 * b + 1]], axis=1)
+                members = range(first, first + GROUP)
+                upcoming = jnp.concatenate([probes[j] for j in members], axis=1)
                 high, low = split(upcoming)
                 crossed = dot(left, jnp.concatenate([high, low, high], axis=0))
                 weights = []
-                for u in range(2):
-                    target_row, target_col, target_tile = place_of(
-                        rows_ref[pl.ds(order_ref[2 * b + u], 1), :]
-                    )
+                for j in members:
+                    target_row, target_col, target_tile = place_of(rows_ref[pl.ds(order_ref[j], 1), :])
                     weight = tapered_weight(from_row, from_col, target_row, target_col, circle)
                     apart = jnp.abs(from_tile - target_tile)
                     near = (apart < 1.5) | (apart > axis_size - 1.5)
                     weights.append(jnp.where(near, weight * scale, 0.0))
-                tapered = crossed * jnp.concatenate(weights, axis=1)
-                high, low = split(tapered)
+                high, low = split(crossed * jnp.concatenate(weights, axis=1))
                 upcoming = upcoming + dot(gains, jnp.concatenate([high, low, high], axis=0))
-                probes[2 * b] = upcoming[:, :obs]
-                probes[2 * b + 1] = upcoming[:, obs:]
-
-            return carry
-
-        for b in range(batches // 2):
-            renew(b, 0)
+                for n, j in enumerate(members):
+                    probes[j] = upcoming[:, n * obs : (n + 1) * obs]
+
+        for first in range(0, batches, GROUP):
+            renew(first)
 
         listed = list_cols[block]
         chosen = lanes[:slots].astype(f32) == listed
@@ -260,15 +264,25 @@
 
 
 def gather_kernel(
-    x_ref, cell_ref, value_ref, noise_ref, weight_ref, landed, table_ref,
-    x_in, mine, tables, packed, partial, total, x_sem,
+    x_ref, cell_hbm, value_hbm, noise_hbm, weight_hbm, landed, table_ref,
+    x_in, cell_ref, value_ref, noise_ref, weight_ref, small_sem, mine, tables, packed, partial, total, x_sem,
     table_send, table_recv, pair_send, pair_recv, send_sem, recv_sem, pass_send, pass_recv,
     *, ranks, cores, batches, mem, levels, cells, obs, own_max,
 ):
     lon, lev = lax.axis_index("lon"), lax.axis_index("lev")
     mesh_id = pl.DeviceIdType.MESH
     fetch = pltpu.make_async_copy(x_ref, x_in, x_sem)
+    small = [
+        pltpu.make_async_copy(src, dst, small_sem.at[i])
+        for i, (src, dst) in enumerate(
+            [(cell_hbm, cell_ref), (value_hbm, value_ref), (noise_hbm, noise_ref), (weight_hbm, weight_ref)]
+        )
+    ]
+    for copy in small:
+        copy.start()
     fetch.start()
+    for copy in small[:3]:
+        copy.wait()
     own = cell_ref.shape[0]
     depth = mine.shape[0]
     row = jnp.concatenate(
@@ -339,6 +353,7 @@
     taken = (wide_code == slot) & (lane < batches * own_max)
     chosen = jnp.where(taken, 1.0, 0.0)
     column = jnp.sum(jnp.where(taken, wide_upper * LON_DEV + wide_lower, 0.0), axis=0, keepdims=True)
+    small[3].wait()
     weighed = jnp.dot(
         weight_ref[...].reshape(batches * levels, obs), chosen, precision=highest, preferred_element_type=f32
     )
@@ -434,7 +449,7 @@
     width = -(-(-(-batches // cores) * mem) // 128) * 128
     depth = -(-own // 8) * 8
     vmem = pl.BlockSpec(memory_space=pltpu.VMEM)
-    hbm = pl.BlockSpec(memory_space=pl.ANY)
+    hbm = pl.BlockSpec(memory_space=pltpu.HBM)
     dma = pltpu.SemaphoreType.DMA
     landed, table = pl.pallas_call(
         functools.partial(
@@ -444,10 +459,15 @@
         out_shape=[
             jax.ShapeDtypeStruct((ranks, cores, own_max, width), f32), jax.ShapeDtypeStruct((obs, 128), f32)
         ],
-        in_specs=[hbm] + [vmem] * 4,
+        in_specs=[hbm] * 5,
         out_specs=[vmem, vmem],
         scratch_shapes=[
             pltpu.VMEM((mem, levels, cells), f32),
+            pltpu.VMEM((own, batches), jnp.int32),
+            pltpu.VMEM((own, batches), f32),
+            pltpu.VMEM((own, batches), f32),
+            pltpu.VMEM((batches, levels, obs), f32),
+            dma((4,)),
             pltpu.VMEM((depth, 128), f32),
             pltpu.VMEM((ranks, depth, 128), f32),
             pltpu.VMEM((cores, own_max, width), f32),
@@ -457,7 +477,7 @@
             dma((cores, ranks)), dma((cores, ranks)),
         ],
         compiler_params=pltpu.CompilerParams(
-            collective_id=0, has_side_effects=True, vmem_limit_bytes=40 * 1024 * 1024
+            collective_id=0, has_side_effects=True, vmem_limit_bytes=67000000
         ),
         name="gather",
     )(ensemble, obs_cell.T, obs_value.T, obs_noise.T, obs_weight)
@@ -468,7 +488,7 @@
             axis_size=ranks, own_max=own_max,
         ),
         out_shape=jax.ShapeDtypeStruct((mem, levels, cells), f32),
-        in_specs=[pl.BlockSpec(memory_space=pltpu.SMEM), hbm, vmem, vmem, vmem],
+        in_specs=[pl.BlockSpec(memory_space=pltpu.SMEM), hbm, vmem, vmem, hbm],
         out_specs=hbm,
         scratch_shapes=[
             pltpu.VMEM((levels, mem, cells), f32),
@@ -483,10 +503,12 @@
             pltpu.VMEM((batches, obs, obs), f32),
             pltpu.VMEM((batches, obs, obs), f32),
             pltpu.VMEM((batches, slots, obs), f32),
+            pltpu.VMEM(tile_lists.shape, jnp.int32),
+            dma(()),
             dma((levels,)),
             dma((levels,)),
         ],
-        compiler_params=pltpu.CompilerParams(vmem_limit_bytes=40 * 1024 * 1024),
+        compiler_params=pltpu.CompilerParams(vmem_limit_bytes=67000000),
         name="assimilate",
     )(batch_order, ensemble, landed, table, tile_lists)
 

time: 118 us -> 113 us (0.958)
  local copies, waits for them, and re-layouts: 4.62 us -> 0 us
    unnamed x14 -> x0, local copies, waits for them, and re-layouts: 4.62 us -> none
    pallas_call x1, Pallas kernels: 90.8 us -> 88.5 us  [body(): pl.pallas_call(functools.partial(kernel_body, batches=batches, levels=lev...]
    pallas_call x1, Pallas kernels: 22.5 us -> 24 us  [body(): pl.pallas_call(functools.partial(gather_kernel, ranks=ranks, cores=cores,...]
where the time goes in v3:
time: 113 us; the launch traced here: 112 us
  Pallas kernels  112 us (99%)
    pallas_call x1, Pallas kernels, body(): pl.pallas_call(functools.partial(kernel_body, batches=batches, levels=lev...  88.5 us
    pallas_call x1, Pallas kernels, body(): pl.pallas_call(functools.partial(gather_kernel, ranks=ranks, cores=cores,...  24 us

profile of v3, /device:TPU:9, one launch (start us, length us, event | category | flops | bytes accessed | tf_op | source)
XLA Modules:
  0.0 112.5 jit_solution(4684415272322793842)
XLA Ops:
  0.0 24.0 %gather.1 = (f32[16,2,8,512]{3,2,1,0:T(8,128)}, f32[128,128]{1,0:T(8,128)}) custom-call(f32[80,8,1024]{2,1,0:T(8,128)} %x_ref.3, s32[8,12]{1,0:T(8,128)} %bitcast.3, f32[8,12]{1,0:T(8,128)} %bitcast.4, f32[8,12]{1,0:T(8,128)} %bitcast.5, f32[12,8,128]{2,1,0:T(8,128)} %weight_hbm.1), custom_call_target="tpu_custom_call" | custom-call | tf_op jit(solution)/shard_map/gather/pallas_call | solution.py:454
  24.0 88.5 %assimilate.1 = f32[80,8,1024]{2,1,0:T(8,128)} custom-call(s32[12]{0:T(128)} %order_ref.1, f32[80,8,1024]{2,1,0:T(8,128)} %x_ref.3, f32[16,2,8,512]{3,2,1,0:T(8,128)} %get-tuple-element.7.landed_ref, f32[128,128]{1,0:T(8,128)} %get-tuple-element.8.table_ref, s32[12,24]{1,0:T(8,128)} %list_hbm.1), custom_call_target="tpu_custom_call" | custom-call | tf_op jit(solution)/shard_map/assimilate/pallas_call | solution.py:485

commit v4 on v3

--- a/solution.py
+++ b/solution.py
@@ -10,6 +10,7 @@
 LON_DEV = 16
 CELL_DEV = 1024
 PANEL = 16
+HALF = 8
 GROUP = 2
 
 highest = lax.Precision.HIGHEST
@@ -34,64 +35,93 @@
     return jnp.exp((e * e + d * d) * (-2.0 / (LON_DEV * LON_DEV)))
 
 
-def eliminate(a_ref, b_ref, noise_root, mem, obs, width, beside):
-    lane = lax.broadcasted_iota(jnp.int32, (1, obs), 1)
-    sample = lax.broadcasted_iota(jnp.int32, (1, width), 1) < mem
-    for start in range(0, obs, PANEL):
-        spot = [[None] * PANEL for _ in range(PANEL)]
-        for i in range(PANEL):
-            for s in range(i + 1):
-                spot[i][s] = jnp.broadcast_to(
-                    a_ref[start + i : start + i + 1, start + s : start + s + 1], (1, obs)
-                )
-        in_panel = (lane >= start) & (lane < start + PANEL)
-        rows = []
-        sides = []
-        for i in range(PANEL):
-            row = a_ref[start + i : start + i + 1, :]
-            rows.append(jnp.where(in_panel, jnp.where(lane == start + i, 1.0, 0.0), row))
-            sides.append(b_ref[start + i : start + i + 1, :])
-        scaled_rows = []
-        scaled_sides = []
-        for r in range(PANEL):
+def eliminate(a_ref, b_ref, root_ref, col_ref, two_ref, low_a, low_b, up_ref, right_ref, mem, obs, beside):
+    lane = lax.broadcasted_iota(jnp.int32, (HALF, obs), 1)
+    sub = lax.broadcasted_iota(jnp.int32, (HALF, obs), 0)
+    sample = lane < mem
+
+    def every(ref, row):
+        return ref[pl.ds(row, HALF, stride=0), :]
+
+    def along(rows, column):
+        return jnp.broadcast_to(rows[:, column : column + 1], (HALF, obs))
+
+    def factor_half(spot, rows, sides, first, base, end, on_pivot):
+        for r in range(HALF):
             pivot = spot[r][r]
             inverse_root = lax.rsqrt(pivot)
             inverse = inverse_root * inverse_root
             root = pivot * inverse_root
-            added = jnp.where(sample, noise_root[start + r], 0.0)
-            factor = 1.0 / (root + added)
-            below = [spot[i][r] * inverse for i in range(r + 1, PANEL)]
-            for n, i in enumerate(range(r + 1, PANEL)):
-                for s in range(r + 1, i + 1):
-                    spot[i][s] = spot[i][s] - below[n] * spot[s][r]
-            solved = sides[r] * factor
+            below = [spot[i][r] * inverse for i in range(r + 1, HALF)]
+            for n, i in enumerate(range(r + 1, HALF)):
+                for t in range(r + 1, i + 1):
+                    spot[i][t] = spot[i][t] - below[n] * spot[t][r]
+            added = jnp.where(sample, every(root_ref, base + r), 0.0)
+            solved = sides[r] * (1.0 / (root + added))
             passing = solved * root
-            for n, i in enumerate(range(r + 1, PANEL)):
+            for n, i in enumerate(range(r + 1, HALF)):
                 rows[i] = rows[i] - below[n] * rows[r]
                 sides[i] = sides[i] - below[n] * passing
-            scaled_rows.append(rows[r] * inverse)
-            scaled_sides.append(solved * inverse_root)
-            a_ref[start + r : start + r + 1, :] = jnp.where(
-                lane < start + PANEL, rows[r] * inverse_root, 0.0
-            )
-            b_ref[start + r : start + r + 1, :] = solved
+            on_pivot(r, spot, inverse, rows[r], passing)
+            at = first + r
+            up_ref[at : at + 1, :] = rows[r][:1]
+            right_ref[at : at + 1, :obs] = (rows[r] * inverse)[:1]
+            right_ref[at : at + 1, obs:] = (solved * inverse_root)[:1]
+            a_ref[base + r : base + r + 1, :] = jnp.where(lane < end, rows[r] * inverse_root, 0.0)[:1]
+            b_ref[base + r : base + r + 1, :] = solved[:1]
+
+    for start in range(0, obs, PANEL):
+        end = start + PANEL
+        middle = start + HALF
+        in_panel = (lane >= start) & (lane < end)
+        raw = [every(a_ref, start + i) for i in range(HALF)]
+        spot = [[along(raw[i], start + t) for t in range(i + 1)] for i in range(HALF)]
+        rows = [jnp.where(in_panel, jnp.where(lane == start + i, 1.0, 0.0), raw[i]) for i in range(HALF)]
+        sides = [every(b_ref, start + i) for i in range(HALF)]
+        rest = a_ref[middle:end, :]
+        column = [along(rest, start + t) for t in range(HALF)]
+        second = [along(rest, middle + t) for t in range(HALF)]
+        state = [
+            jnp.where(in_panel, jnp.where(lane == middle + sub, 1.0, 0.0), rest),
+            b_ref[middle:end, :],
+        ]
+
+        def reach(r, spot, inverse, row, passing):
+            col_ref[HALF * r : HALF * r + HALF, :] = column[r]
+            scaled = column[r] * inverse
+            for t in range(r + 1, HALF):
+                column[t] = column[t] - scaled * spot[t][r]
+            state[0] = state[0] - scaled * row
+            state[1] = state[1] - scaled * passing
+            for t in range(HALF):
+                second[t] = second[t] - scaled * every(col_ref, HALF * r + t)
+
+        factor_half(spot, rows, sides, 0, start, end, reach)
+        for t in range(HALF):
+            two_ref[HALF * t : HALF * t + HALF, :] = second[t]
+        low_a[...] = state[0]
+        low_b[...] = state[1]
+        spot = [[every(two_ref, HALF * t + i) for t in range(i + 1)] for i in range(HALF)]
+        rows = [every(low_a, i) for i in range(HALF)]
+        sides = [every(low_b, i) for i in range(HALF)]
+        factor_half(spot, rows, sides, HALF, middle, end, lambda *unused: None)
         beside(start // PANEL, obs // PANEL)
-        after = start + PANEL
-        if after < obs:
-            u_high, u_low = split(jnp.concatenate(rows, axis=0))
-            high, low = split(jnp.concatenate(
-                [jnp.concatenate(scaled_rows, axis=0), jnp.concatenate(scaled_sides, axis=0)], axis=1
-            ))
+        if end < obs:
+            u_high, u_low = split(up_ref[...])
+            high, low = split(right_ref[...])
             upper = jnp.concatenate([u_high.astype(f32), u_high.astype(f32), u_low.astype(f32)], axis=0)
-            left = upper.T.astype(bf16)[after:, :]
+            left = upper.T.astype(bf16)[end:, :]
             change = dot(left, jnp.concatenate([high, low, high], axis=0))
-            a_ref[after:, :] = jnp.where(in_panel, 0.0, a_ref[after:, :]) - change[:, :obs]
-            b_ref[after:, :] = b_ref[after:, :] - change[:, obs:]
+            a_ref[end:, :] = jnp.where(
+                (lane[:1] >= start) & (lane[:1] < end), 0.0, a_ref[end:, :]
+            ) - change[:, :obs]
+            b_ref[end:, :] = b_ref[end:, :] - change[:, obs:]
 
 
 def kernel_body(
     order_ref, x_ref, landed_ref, table_ref, list_hbm, out_ref,
-    state, natural, probes, a_ref, b_ref, weight_ref, left_ref, gains_ref, rows_ref, noise_cols, cell_cols,
+    state, natural, probes, a_ref, b_ref, root_ref, col_ref, two_ref, low_a, low_b, up_ref,
+    right_ref, weight_ref, left_ref, gains_ref, rows_ref, noise_cols, cell_cols,
     list_cols, list_ref, sem_list, sem_in, sem_out, *, batches, levels, mem, obs, cells, slots, axis_size, own_max,
 ):
     def fetch(level):
@@ -188,9 +218,8 @@
         covariance = dot(left, jnp.concatenate([s_high, s_low, s_high], axis=0)) * scale
         a_ref[...] = covariance + jnp.where(lanes == subs, noise_row, 0.0)
         b_ref[...] = sides
-        root_col = noise_cols[block]
-        roots = [root_col[j : j + 1, :] for j in range(obs)]
-        eliminate(a_ref, b_ref, roots, mem, obs, obs, beside)
+        root_ref[...] = noise_cols[block]
+        eliminate(a_ref, b_ref, root_ref, col_ref, two_ref, low_a, low_b, up_ref, right_ref, mem, obs, beside)
         f_high, f_low = split(a_ref[...].T)
         b_high, b_low = split(b_ref[...])
         joined = dot(
@@ -496,6 +525,13 @@
             pltpu.VMEM((batches, mem, obs), f32),
             pltpu.VMEM((obs, obs), f32),
             pltpu.VMEM((obs, obs), f32),
+            pltpu.VMEM((obs, obs), f32),
+            pltpu.VMEM((HALF * HALF, obs), f32),
+            pltpu.VMEM((HALF * HALF, obs), f32),
+            pltpu.VMEM((HALF, obs), f32),
+            pltpu.VMEM((HALF, obs), f32),
+            pltpu.VMEM((PANEL, obs), f32),
+            pltpu.VMEM((PANEL, 2 * obs), f32),
             pltpu.VMEM((slots, cells), f32),
             pltpu.VMEM((slots, 3 * mem), bf16),
             pltpu.VMEM((mem, 3 * slots), bf16),

time: 113 us -> 101 us (0.89)
  Pallas kernels: 112 us -> 100 us
    pallas_call x1, Pallas kernels: 88.5 us -> 76.5 us  [body(): pl.pallas_call(functools.partial(kernel_body, batches=batches, levels=lev...]
where the time goes in v4:
time: 101 us; the launch traced here: 100 us
  Pallas kernels  100 us (99%)
    pallas_call x1, Pallas kernels, body(): pl.pallas_call(functools.partial(kernel_body, batches=batches, levels=lev...  76.5 us
    pallas_call x1, Pallas kernels, body(): pl.pallas_call(functools.partial(gather_kernel, ranks=ranks, cores=cores,...  24 us

profile of v4, /device:TPU:9, one launch (start us, length us, event | category | flops | bytes accessed | tf_op | source)
XLA Modules:
  0.0 100.4 jit_solution(2542004287955948633)
XLA Ops:
  0.0 24.0 %gather.1 = (f32[16,2,8,512]{3,2,1,0:T(8,128)}, f32[128,128]{1,0:T(8,128)}) custom-call(f32[80,8,1024]{2,1,0:T(8,128)} %x_ref.3, s32[8,12]{1,0:T(8,128)} %bitcast.3, f32[8,12]{1,0:T(8,128)} %bitcast.4, f32[8,12]{1,0:T(8,128)} %bitcast.5, f32[12,8,128]{2,1,0:T(8,128)} %weight_hbm.1), custom_call_target="tpu_custom_call" | custom-call | tf_op jit(solution)/shard_map/gather/pallas_call | solution.py:483
  24.0 76.5 %assimilate.1 = f32[80,8,1024]{2,1,0:T(8,128)} custom-call(s32[12]{0:T(128)} %order_ref.1, f32[80,8,1024]{2,1,0:T(8,128)} %x_ref.3, f32[16,2,8,512]{3,2,1,0:T(8,128)} %get-tuple-element.7.landed_ref, f32[128,128]{1,0:T(8,128)} %get-tuple-element.8.table_ref, s32[12,24]{1,0:T(8,128)} %list_hbm.1), custom_call_target="tpu_custom_call" | custom-call | tf_op jit(solution)/shard_map/assimilate/pallas_call | solution.py:514
